TPU v7x, 128 devices: a whole 4x4x4 slice. The times are simulated.
128 devices in a mesh: lat: 4 (over y_hi, core), lon: 4 (over z_hi, y_lo), lev: 8 (over z_lo, x).
Axes of the slice: x: 4, y: 4 (y_hi: 2, y_lo: 2; y = y_hi * 2 + y_lo), z: 4 (z_hi: 2, z_lo: 2; z = z_hi * 2 + z_lo), core: 2. Of those that a mesh axis runs over, the one named last changes fastest.
Arguments:
- density: float32 [128, 16, 1024, 128], P('lat', 'lon', 'lev'), may hold values from 0.2 to 1.8
- crowding: float32 [128, 16, 1024, 128], P('lat', 'lon', 'lev'), may hold values from 0.5 to 2
Outputs:
- running_total: float32 [128, 16, 1024, 128], P('lat', 'lon', 'lev')
- density_end: float32 [128, 16, 1024, 128], P('lat', 'lon', 'lev')
All inputs are finite; a program needn't handle non-finite values.
Results may differ from a plain program's by a relative error of at most 0.00002.
Values sent between devices are 32-bit elements; how exact they have to be, the bound alone decides.
A program may use at most 320 MiB of HBM per device.

v0:
```python
import jax
import jax.numpy as jnp
from jax import lax
from jax.sharding import Mesh
from jax.sharding import PartitionSpec as P

STEPS = 4
LON = ("lon_0", "lon_1")


def padded_2(value, sides, width):
    edges = {}
    for axis, dim in sides:
        devices, length = (lax.axis_size(axis), value.shape[dim])
        up = [(i, (i + 1) % devices) for i in range(devices)]
        last = lax.slice_in_dim(value, length - width, length, axis=dim)
        leading = lax.slice_in_dim(value, 0, width, axis=dim)
        edges[dim] = (
            lax.ppermute(last, axis, up),
            lax.ppermute(leading, axis, [(b, a) for a, b in up]),
        )
    done = []
    for _, dim in sides:
        low, high = edges[dim]
        around = [(width, width) if d in done else (0, 0) for d in range(value.ndim)]
        value = jnp.concatenate([jnp.pad(low, around), value, jnp.pad(high, around)], axis=dim)
        done.append(dim)
    return value


def nothing_yet(value, identity):
    return jnp.broadcast_to(jnp.asarray(identity, value.dtype), value.shape)


def prefix_by_axis(value, axes, combine, identity):
    before = start = nothing_yet(value, identity)
    so_far = value
    for axis in reversed(axes):
        devices, place = (lax.axis_size(axis), lax.axis_index(axis))
        pieces = lax.all_gather(so_far, axis)
        inside, so_far = (start, start)
        for k in range(devices):
            passed = k < place
            so_far = combine(so_far, pieces[k])
            inside = jnp.where(passed, so_far, inside)
        before = combine(inside, before)
    return before


def without_rim(values, dims):
    for dim in dims:
        values = lax.slice_in_dim(values, 1, values.shape[dim] - 1, axis=dim)
    return values


def shifted_cells(values, dim, start, dims):
    others = [other for other in dims if other != dim]
    values = without_rim(values, others)
    return lax.slice_in_dim(values, start, start + values.shape[dim] - 2, axis=dim)


def march_step(padded, crowding):
    middle = without_rim(padded, (0, 1, 2))
    lower = [shifted_cells(padded, dim, 0, (0, 1, 2)) for dim in (0, 1, 2)]
    upper = [shifted_cells(padded, dim, 2, (0, 1, 2)) for dim in (0, 1, 2)]
    spread = lower[0] + upper[0] + lower[1] + upper[1] + lower[2] + upper[2] - 6.0 * middle
    return middle + 0.1 * spread + 0.2 * middle * (1.0 - middle * crowding)


def body(density, crowding):
    for step in range(STEPS):
        padded = padded_2(density, (("lat", 0), (LON, 1), ("lev", 2)), 1)
        density = march_step(padded, crowding)
    here = jnp.cumsum(density, axis=1)
    total = lax.slice_in_dim(here, here.shape[1] - 1, here.shape[1], axis=1)

    def add_pair(earlier_total, later_total):
        return earlier_total + later_total

    below = prefix_by_axis(total, LON, add_pair, jnp.zeros_like(total))
    running_total = (here + below) / (density.shape[1] * lax.axis_size(LON))
    return (running_total, density)


def solution(mesh):
    finer = Mesh(
        mesh.devices.reshape(mesh.shape["lat"], 2, 2, mesh.shape["lev"]),
        ("lat", "lon_0", "lon_1", "lev"),
    )
    return jax.shard_map(
        body,
        mesh=finer,
        in_specs=(P("lat", LON, "lev", None), P("lat", LON, "lev", None)),
        out_specs=(P("lat", LON, "lev", None), P("lat", LON, "lev", None)),
        check_vma=False,
    )
```

profile of v0, /device:TPU:0, one launch (start us, length us, event | category | flops | bytes accessed | tf_op | source)
XLA Modules:
  0.0 712.9 jit_solution(9351725978303792233)
XLA Ops:
  7.2 5.0 fusion.57
  12.2 1.7 collective-permute-start.2
  13.9 3.3 collective-permute-start.3
  17.3 0.1 collective-permute-start
  17.4 3.2 collective-permute-start.1
  20.6 0.1 fusion.56
  20.7 1.6 collective-permute-start.4
  22.3 89.5 %collective-permute-done = f32[1,4,128,128]{3,2,1,0:T(8,128)S(1)} collective-permute-done((f32[1,4,128,128]{3,2,1,0:T(8,128)S(1)}, f32[1,4,128,128]{3,2,1,0:T(8,128)S(1)}, u32[]{:S(2)}, u32[]{:S(2)}) %collective-permute-start) | collective-permute-done | bytes 262176 | tf_op jit(solution)/shard_map/ppermute | solution.py:19
  111.8 4.1 collective-permute-start.5
  115.9 0.7 constant_dynamic-update-slice_fusion.2
  116.6 4.9 constant_dynamic-update-slice_fusion.1
  121.5 0.7 constant_dynamic-update-slice_fusion
  122.2 1.6 pad.50
  123.8 1.6 pad.51
  125.5 29.7 %fusion.38 = f32[32,4,128,128]{3,2,1,0:T(8,128)} fusion(f32[32,4,128,128]{3,2,1,0:T(8,128)} %param.2, f32[32,4,1,128]{3,2,1,0:T(1,128)S(1)} %collective-permute-done.5, f32[34,1,128,128]{3,2,1,0:T(8,128)} %pad.51, f32[34,4,128,128]{3,2,1,0:T(8,128)} %constant_dynamic-update-slice_fusion, f32[34,1,128,128]{3,2,1,0:T(8,128)} %pad.50, ...), kind=kLoop, calls=%fused_computation.93 | loop fusion | flops 62914560 | bytes 39190528 | tf_op jit(solution)/shard_map/add | solution.py:67
  155.2 2.5 fusion.55
  157.7 2.6 collective-permute-start.8
  160.3 1.9 collective-permute-start.9
  162.2 1.1 fusion.54
  163.3 0.1 collective-permute-start.6
  163.3 3.2 collective-permute-start.7
  166.6 1.3 fusion.53
  167.9 0.1 collective-permute-start.10
  168.0 42.0 %collective-permute-done.8 = f32[32,1,128,128]{3,2,1,0:T(8,128)S(1)} collective-permute-done((f32[32,1,128,128]{3,2,1,0:T(8,128)S(1)}, f32[32,1,128,128]{3,2,1,0:T(8,128)S(1)}, u32[]{:S(2)}, u32[]{:S(2)}) %collective-permute-start.8) | collective-permute-done | bytes 2097184 | tf_op jit(solution)/shard_map/ppermute | solution.py:19
  210.0 1.7 pad.54
  211.7 42.2 %collective-permute-done.9 = f32[32,1,128,128]{3,2,1,0:T(8,128)S(1)} collective-permute-done((f32[32,1,128,128]{3,2,1,0:T(8,128)S(1)}, f32[32,1,128,128]{3,2,1,0:T(8,128)S(1)}, u32[]{:S(2)}, u32[]{:S(2)}) %collective-permute-start.9) | collective-permute-done | bytes 2097184 | tf_op jit(solution)/shard_map/ppermute | solution.py:20
  253.9 1.6 pad.55
  255.6 32.5 %fusion.27 = f32[32,4,128,128]{3,2,1,0:T(8,128)} fusion(f32[32,4,128,128]{3,2,1,0:T(8,128)} %fusion.38, f32[32,4,1,128]{3,2,1,0:T(1,128)S(1)} %collective-permute-done.11, f32[34,1,128,128]{3,2,1,0:T(8,128)} %pad.55, f32[34,1,128,128]{3,2,1,0:T(8,128)} %pad.54, f32[1,4,128,128]{3,2,1,0:T(8,128)S(1)} %collective-permute-done.7, ...), kind=kLoop, calls=%fused_computation.64 | loop fusion | flops 79691776 | bytes 30277632 | tf_op jit(solution)/shard_map/add | solution.py:67
  288.1 2.5 fusion.52
  290.6 1.3 collective-permute-start.14
  291.9 3.2 collective-permute-start.15
  295.1 1.1 fusion.51
  296.2 0.1 collective-permute-start.12
  296.3 3.2 collective-permute-start.13
  299.5 1.3 fusion.50
  300.8 0.1 collective-permute-start.16
  300.9 42.0 %collective-permute-done.14 = f32[32,1,128,128]{3,2,1,0:T(8,128)S(1)} collective-permute-done((f32[32,1,128,128]{3,2,1,0:T(8,128)S(1)}, f32[32,1,128,128]{3,2,1,0:T(8,128)S(1)}, u32[]{:S(2)}, u32[]{:S(2)}) %collective-permute-start.14) | collective-permute-done | bytes 2097184 | tf_op jit(solution)/shard_map/ppermute | solution.py:19
  342.9 1.7 pad.58
  344.6 39.1 %collective-permute-done.15 = f32[32,1,128,128]{3,2,1,0:T(8,128)S(1)} collective-permute-done((f32[32,1,128,128]{3,2,1,0:T(8,128)S(1)}, f32[32,1,128,128]{3,2,1,0:T(8,128)S(1)}, u32[]{:S(2)}, u32[]{:S(2)}) %collective-permute-start.15) | collective-permute-done | bytes 2097184 | tf_op jit(solution)/shard_map/ppermute | solution.py:20
  383.7 1.6 pad.59
  385.3 6.0 collective-permute-done.12
  391.3 32.8 %fusion.16 = f32[32,4,128,128]{3,2,1,0:T(8,128)} fusion(f32[32,4,128,128]{3,2,1,0:T(8,128)} %fusion.27, f32[32,4,1,128]{3,2,1,0:T(1,128)S(1)} %collective-permute-done.17, f32[34,1,128,128]{3,2,1,0:T(8,128)} %pad.59, f32[34,1,128,128]{3,2,1,0:T(8,128)} %pad.58, f32[1,4,128,128]{3,2,1,0:T(8,128)S(1)} %collective-permute-done.13, ...), kind=kLoop, calls=%fused_computation.35 | loop fusion | flops 79691776 | bytes 30277632 | tf_op jit(solution)/shard_map/add | solution.py:67
  424.1 2.5 fusion.49
  426.6 0.9 collective-permute-start.20
  427.5 3.6 collective-permute-start.21
  431.1 1.1 fusion.48
  432.2 0.1 collective-permute-start.18
  432.3 3.2 collective-permute-start.19
  435.5 1.3 fusion.47
  436.8 0.1 collective-permute-start.22
  436.9 42.0 %collective-permute-done.20 = f32[32,1,128,128]{3,2,1,0:T(8,128)S(1)} collective-permute-done((f32[32,1,128,128]{3,2,1,0:T(8,128)S(1)}, f32[32,1,128,128]{3,2,1,0:T(8,128)S(1)}, u32[]{:S(2)}, u32[]{:S(2)}) %collective-permute-start.20) | collective-permute-done | bytes 2097184 | tf_op jit(solution)/shard_map/ppermute | solution.py:19
  478.9 1.7 pad.62
  480.6 40.5 %collective-permute-done.21 = f32[32,1,128,128]{3,2,1,0:T(8,128)S(1)} collective-permute-done((f32[32,1,128,128]{3,2,1,0:T(8,128)S(1)}, f32[32,1,128,128]{3,2,1,0:T(8,128)S(1)}, u32[]{:S(2)}, u32[]{:S(2)}) %collective-permute-start.21) | collective-permute-done | bytes 2097184 | tf_op jit(solution)/shard_map/ppermute | solution.py:20
  521.1 1.6 pad.63
  522.7 0.2 collective-permute-done.18
  523.0 32.5 %fusion.5 = f32[32,4,128,128]{3,2,1,0:T(8,128)} fusion(f32[32,4,128,128]{3,2,1,0:T(8,128)} %fusion.16, f32[32,4,1,128]{3,2,1,0:T(1,128)S(1)} %collective-permute-done.23, f32[34,1,128,128]{3,2,1,0:T(8,128)} %pad.63, f32[34,1,128,128]{3,2,1,0:T(8,128)} %pad.62, f32[1,4,128,128]{3,2,1,0:T(8,128)S(1)} %collective-permute-done.19, ...), kind=kLoop, calls=%fused_computation.6 | loop fusion | flops 79691776 | bytes 30277632 | tf_op jit(solution)/shard_map/add | solution.py:67
  555.5 8.4 %fusion.59 = f32[32,4,128,128]{3,2,1,0:T(8,128)} fusion(f32[32,4,128,128]{3,2,1,0:T(8,128)} %fusion.5), kind=kOutput, calls=%fused_computation.131 | output fusion | flops 6291456 | bytes 16777216 | tf_op jit(solution)/shard_map/jit(cumsum)/reduce_window_sum | solution.py:74
  563.9 3.2 slice.390
  567.1 0.0 all-gather.7.cloned.1.call-start
  567.1 59.9 %all-gather.5.cloned.1.call-done = f32[64,1,128,128]{3,2,1,0:T(8,128)} async-done(((f32[32,1,128,128]{3,2,1,0:T(8,128)}), f32[64,1,128,128]{3,2,1,0:T(8,128)}) %all-gather.5.cloned.1.call-update) | async-done | bytes 4194320 | tf_op jit(solution)/shard_map/all_gather | solution.py:40
  627.0 3.9 slice_add_fusion.1
  630.9 62.0 %all-gather.7.cloned.1.call-done = f32[64,1,128,128]{3,2,1,0:T(8,128)} async-done(((f32[32,1,128,128]{3,2,1,0:T(8,128)}), f32[64,1,128,128]{3,2,1,0:T(8,128)}) %all-gather.7.cloned.1.call-update) | async-done | bytes 4194320 | tf_op jit(solution)/shard_map/all_gather | solution.py:40
  693.0 4.4 fusion.46
  697.3 8.7 %add_multiply_fusion = f32[32,4,128,128]{3,2,1,0:T(8,128)} fusion(f32[32,4,128,128]{3,2,1,0:T(8,128)} %fusion.59, f32[32,128,128]{2,1,0:T(8,128)S(1)} %fusion.46), kind=kLoop, calls=%fused_computation.110 | loop fusion | flops 4194304 | bytes 18874368 | tf_op jit(solution)/shard_map/div | solution.py:81
  (29 shorter events, 0.2 us)
Async XLA Ops:
  7.2 619.8 %all-gather.5.cloned.1.call-start = ((), (), s32[]{:S(2)}) async-start(), calls=%async_computation | async-start | bytes 6291456 | tf_op jit(solution)/shard_map/all_gather | solution.py:40
  7.2 10.0 %copy-start = (f32[32,4,128,128]{3,2,1,0:T(8,128)S(1)}, f32[32,4,128,128]{3,2,1,0:T(8,128)}, u32[]{:S(2)}) copy-start(f32[32,4,128,128]{3,2,1,0:T(8,128)} %param.2) | copy-start | bytes 25165828
  12.2 110.0 %collective-permute-start.2 = (f32[32,1,128,128]{3,2,1,0:T(8,128)}, f32[32,1,128,128]{3,2,1,0:T(8,128)S(1)}, u32[]{:S(2)}, u32[]{:S(2)}) collective-permute-start(f32[32,1,128,128]{3,2,1,0:T(8,128)} %get-tuple-element.22), channel_id=1, source_target_pairs={{0,8},{8,16},{16,24},{24,0},{1,9},{9,17},{17,25},{25,1},{2,10},{10... | collective-permute-start | bytes 6291464 | tf_op jit(solution)/shard_map/ppermute | solution.py:19
  13.9 109.9 %collective-permute-start.3 = (f32[32,1,128,128]{3,2,1,0:T(8,128)}, f32[32,1,128,128]{3,2,1,0:T(8,128)S(1)}, u32[]{:S(2)}, u32[]{:S(2)}) collective-permute-start(f32[32,1,128,128]{3,2,1,0:T(8,128)} %get-tuple-element.23), channel_id=1, source_target_pairs={{8,0},{16,8},{24,16},{0,24},{9,1},{17,9},{25,17},{1,25},{10,2},{18... | collective-permute-start | bytes 6291464 | tf_op jit(solution)/shard_map/ppermute | solution.py:20
  17.3 94.5 %collective-permute-start = (f32[1,4,128,128]{3,2,1,0:T(8,128)S(1)}, f32[1,4,128,128]{3,2,1,0:T(8,128)S(1)}, u32[]{:S(2)}, u32[]{:S(2)}) collective-permute-start(f32[1,4,128,128]{3,2,1,0:T(8,128)S(1)} %get-tuple-element.25), channel_id=1, source_target_pairs={{0,32},{32,64},{64,96},{96,0},{1,33},{33,65},{65,97},{97,1},{2,34}... | collective-permute-start | bytes 786440 | tf_op jit(solution)/shard_map/ppermute | solution.py:19
  17.4 104.1 %collective-permute-start.1 = (f32[1,4,128,128]{3,2,1,0:T(8,128)S(1)}, f32[1,4,128,128]{3,2,1,0:T(8,128)S(1)}, u32[]{:S(2)}, u32[]{:S(2)}) collective-permute-start(f32[1,4,128,128]{3,2,1,0:T(8,128)S(1)} %get-tuple-element.24), channel_id=1, source_target_pairs={{32,0},{64,32},{96,64},{0,96},{33,1},{65,33},{97,65},{1,97},{34,2}... | collective-permute-start | bytes 786440 | tf_op jit(solution)/shard_map/ppermute | solution.py:20
  20.7 104.8 %collective-permute-start.4 = (f32[32,4,1,128]{3,2,1,0:T(1,128)S(1)}, f32[32,4,1,128]{3,2,1,0:T(1,128)S(1)}, u32[]{:S(2)}, u32[]{:S(2)}) collective-permute-start(f32[32,4,1,128]{3,2,1,0:T(1,128)S(1)} %get-tuple-element.20), channel_id=1, source_target_pairs={{0,1},{1,2},{2,3},{3,4},{4,5},{5,6},{6,7},{7,0},{8,9},{9,10},{10,1... | collective-permute-start | bytes 196616 | tf_op jit(solution)/shard_map/ppermute | solution.py:19
  111.8 13.7 %collective-permute-start.5 = (f32[32,4,1,128]{3,2,1,0:T(1,128)S(1)}, f32[32,4,1,128]{3,2,1,0:T(1,128)S(1)}, u32[]{:S(2)}, u32[]{:S(2)}) collective-permute-start(f32[32,4,1,128]{3,2,1,0:T(1,128)S(1)} %get-tuple-element.21), channel_id=1, source_target_pairs={{1,0},{2,1},{3,2},{4,3},{5,4},{6,5},{7,6},{0,7},{9,8},{10,9},{11,1... | collective-permute-start | bytes 196616 | tf_op jit(solution)/shard_map/ppermute | solution.py:20
  115.9 9.6 %slice-start = ((s8[8388608]{0:T(1024)(128)(4,1)}), s8[4194304]{0:T(1024)(128)(4,1)S(1)}, s32[]{:S(2)}) async-start(s8[8388608]{0:T(1024)(128)(4,1)} %bitcast.3), calls=%async_computation.2 | async-start | bytes 8388608
  116.6 8.9 %slice-start.1 = ((s8[8388608]{0:T(1024)(128)(4,1)}), s8[4194304]{0:T(1024)(128)(4,1)S(1)}, s32[]{:S(2)}) async-start(s8[8388608]{0:T(1024)(128)(4,1)} %bitcast.3), calls=%async_computation.3 | async-start | bytes 8388608
  157.7 52.3 %collective-permute-start.8 = (f32[32,1,128,128]{3,2,1,0:T(8,128)S(1)}, f32[32,1,128,128]{3,2,1,0:T(8,128)S(1)}, u32[]{:S(2)}, u32[]{:S(2)}) collective-permute-start(f32[32,1,128,128]{3,2,1,0:T(8,128)S(1)} %get-tuple-element.18), channel_id=1, source_target_pairs={{0,8},{8,16},{16,24},{24,0},{1,9},{9,17},{17,25},{25,1},{2,10},{10... | collective-permute-start | bytes 6291464 | tf_op jit(solution)/shard_map/ppermute | solution.py:19
  160.3 93.6 %collective-permute-start.9 = (f32[32,1,128,128]{3,2,1,0:T(8,128)S(1)}, f32[32,1,128,128]{3,2,1,0:T(8,128)S(1)}, u32[]{:S(2)}, u32[]{:S(2)}) collective-permute-start(f32[32,1,128,128]{3,2,1,0:T(8,128)S(1)} %get-tuple-element.19), channel_id=1, source_target_pairs={{8,0},{16,8},{24,16},{0,24},{9,1},{17,9},{25,17},{1,25},{10,2},{18... | collective-permute-start | bytes 6291464 | tf_op jit(solution)/shard_map/ppermute | solution.py:20
  163.3 92.3 %collective-permute-start.6 = (f32[1,4,128,128]{3,2,1,0:T(8,128)S(1)}, f32[1,4,128,128]{3,2,1,0:T(8,128)S(1)}, u32[]{:S(2)}, u32[]{:S(2)}) collective-permute-start(f32[1,4,128,128]{3,2,1,0:T(8,128)S(1)} %get-tuple-element.16), channel_id=1, source_target_pairs={{0,32},{32,64},{64,96},{96,0},{1,33},{33,65},{65,97},{97,1},{2,34}... | collective-permute-start | bytes 786440 | tf_op jit(solution)/shard_map/ppermute | solution.py:19
  163.3 92.2 %collective-permute-start.7 = (f32[1,4,128,128]{3,2,1,0:T(8,128)S(1)}, f32[1,4,128,128]{3,2,1,0:T(8,128)S(1)}, u32[]{:S(2)}, u32[]{:S(2)}) collective-permute-start(f32[1,4,128,128]{3,2,1,0:T(8,128)S(1)} %get-tuple-element.17), channel_id=1, source_target_pairs={{32,0},{64,32},{96,64},{0,96},{33,1},{65,33},{97,65},{1,97},{34,2}... | collective-permute-start | bytes 786440 | tf_op jit(solution)/shard_map/ppermute | solution.py:20
  167.9 87.6 %collective-permute-start.10 = (f32[32,4,1,128]{3,2,1,0:T(1,128)S(1)}, f32[32,4,1,128]{3,2,1,0:T(1,128)S(1)}, u32[]{:S(2)}, u32[]{:S(2)}) collective-permute-start(f32[32,4,1,128]{3,2,1,0:T(1,128)S(1)} %get-tuple-element.14), channel_id=1, source_target_pairs={{0,1},{1,2},{2,3},{3,4},{4,5},{5,6},{6,7},{7,0},{8,9},{9,10},{10,1... | collective-permute-start | bytes 196616 | tf_op jit(solution)/shard_map/ppermute | solution.py:19
  210.0 45.5 %collective-permute-start.11 = (f32[32,4,1,128]{3,2,1,0:T(1,128)S(1)}, f32[32,4,1,128]{3,2,1,0:T(1,128)S(1)}, u32[]{:S(2)}, u32[]{:S(2)}) collective-permute-start(f32[32,4,1,128]{3,2,1,0:T(1,128)S(1)} %get-tuple-element.15), channel_id=1, source_target_pairs={{1,0},{2,1},{3,2},{4,3},{5,4},{6,5},{7,6},{0,7},{9,8},{10,9},{11,1... | collective-permute-start | bytes 196616 | tf_op jit(solution)/shard_map/ppermute | solution.py:20
  290.6 52.3 %collective-permute-start.14 = (f32[32,1,128,128]{3,2,1,0:T(8,128)S(1)}, f32[32,1,128,128]{3,2,1,0:T(8,128)S(1)}, u32[]{:S(2)}, u32[]{:S(2)}) collective-permute-start(f32[32,1,128,128]{3,2,1,0:T(8,128)S(1)} %get-tuple-element.12), channel_id=1, source_target_pairs={{0,8},{8,16},{16,24},{24,0},{1,9},{9,17},{17,25},{25,1},{2,10},{10... | collective-permute-start | bytes 6291464 | tf_op jit(solution)/shard_map/ppermute | solution.py:19
  291.9 91.8 %collective-permute-start.15 = (f32[32,1,128,128]{3,2,1,0:T(8,128)S(1)}, f32[32,1,128,128]{3,2,1,0:T(8,128)S(1)}, u32[]{:S(2)}, u32[]{:S(2)}) collective-permute-start(f32[32,1,128,128]{3,2,1,0:T(8,128)S(1)} %get-tuple-element.13), channel_id=1, source_target_pairs={{8,0},{16,8},{24,16},{0,24},{9,1},{17,9},{25,17},{1,25},{10,2},{18... | collective-permute-start | bytes 6291464 | tf_op jit(solution)/shard_map/ppermute | solution.py:20
  296.2 95.1 %collective-permute-start.12 = (f32[1,4,128,128]{3,2,1,0:T(8,128)S(1)}, f32[1,4,128,128]{3,2,1,0:T(8,128)S(1)}, u32[]{:S(2)}, u32[]{:S(2)}) collective-permute-start(f32[1,4,128,128]{3,2,1,0:T(8,128)S(1)} %get-tuple-element.10), channel_id=1, source_target_pairs={{0,32},{32,64},{64,96},{96,0},{1,33},{33,65},{65,97},{97,1},{2,34}... | collective-permute-start | bytes 786440 | tf_op jit(solution)/shard_map/ppermute | solution.py:19
  296.3 95.0 %collective-permute-start.13 = (f32[1,4,128,128]{3,2,1,0:T(8,128)S(1)}, f32[1,4,128,128]{3,2,1,0:T(8,128)S(1)}, u32[]{:S(2)}, u32[]{:S(2)}) collective-permute-start(f32[1,4,128,128]{3,2,1,0:T(8,128)S(1)} %get-tuple-element.11), channel_id=1, source_target_pairs={{32,0},{64,32},{96,64},{0,96},{33,1},{65,33},{97,65},{1,97},{34,2}... | collective-permute-start | bytes 786440 | tf_op jit(solution)/shard_map/ppermute | solution.py:20
  300.8 84.5 %collective-permute-start.16 = (f32[32,4,1,128]{3,2,1,0:T(1,128)S(1)}, f32[32,4,1,128]{3,2,1,0:T(1,128)S(1)}, u32[]{:S(2)}, u32[]{:S(2)}) collective-permute-start(f32[32,4,1,128]{3,2,1,0:T(1,128)S(1)} %get-tuple-element.8), channel_id=1, source_target_pairs={{0,1},{1,2},{2,3},{3,4},{4,5},{5,6},{6,7},{7,0},{8,9},{9,10},{10,1... | collective-permute-start | bytes 196616 | tf_op jit(solution)/shard_map/ppermute | solution.py:19
  342.9 42.4 %collective-permute-start.17 = (f32[32,4,1,128]{3,2,1,0:T(1,128)S(1)}, f32[32,4,1,128]{3,2,1,0:T(1,128)S(1)}, u32[]{:S(2)}, u32[]{:S(2)}) collective-permute-start(f32[32,4,1,128]{3,2,1,0:T(1,128)S(1)} %get-tuple-element.9), channel_id=1, source_target_pairs={{1,0},{2,1},{3,2},{4,3},{5,4},{6,5},{7,6},{0,7},{9,8},{10,9},{11,1... | collective-permute-start | bytes 196616 | tf_op jit(solution)/shard_map/ppermute | solution.py:20
  426.6 52.3 %collective-permute-start.20 = (f32[32,1,128,128]{3,2,1,0:T(8,128)S(1)}, f32[32,1,128,128]{3,2,1,0:T(8,128)S(1)}, u32[]{:S(2)}, u32[]{:S(2)}) collective-permute-start(f32[32,1,128,128]{3,2,1,0:T(8,128)S(1)} %get-tuple-element.6), channel_id=1, source_target_pairs={{0,8},{8,16},{16,24},{24,0},{1,9},{9,17},{17,25},{25,1},{2,10},{10... | collective-permute-start | bytes 6291464 | tf_op jit(solution)/shard_map/ppermute | solution.py:19
  427.5 93.5 %collective-permute-start.21 = (f32[32,1,128,128]{3,2,1,0:T(8,128)S(1)}, f32[32,1,128,128]{3,2,1,0:T(8,128)S(1)}, u32[]{:S(2)}, u32[]{:S(2)}) collective-permute-start(f32[32,1,128,128]{3,2,1,0:T(8,128)S(1)} %get-tuple-element.7), channel_id=1, source_target_pairs={{8,0},{16,8},{24,16},{0,24},{9,1},{17,9},{25,17},{1,25},{10,2},{18... | collective-permute-start | bytes 6291464 | tf_op jit(solution)/shard_map/ppermute | solution.py:20
  432.2 90.8 %collective-permute-start.18 = (f32[1,4,128,128]{3,2,1,0:T(8,128)S(1)}, f32[1,4,128,128]{3,2,1,0:T(8,128)S(1)}, u32[]{:S(2)}, u32[]{:S(2)}) collective-permute-start(f32[1,4,128,128]{3,2,1,0:T(8,128)S(1)} %get-tuple-element.4), channel_id=1, source_target_pairs={{0,32},{32,64},{64,96},{96,0},{1,33},{33,65},{65,97},{97,1},{2,34}... | collective-permute-start | bytes 786440 | tf_op jit(solution)/shard_map/ppermute | solution.py:19
  432.3 90.7 %collective-permute-start.19 = (f32[1,4,128,128]{3,2,1,0:T(8,128)S(1)}, f32[1,4,128,128]{3,2,1,0:T(8,128)S(1)}, u32[]{:S(2)}, u32[]{:S(2)}) collective-permute-start(f32[1,4,128,128]{3,2,1,0:T(8,128)S(1)} %get-tuple-element.5), channel_id=1, source_target_pairs={{32,0},{64,32},{96,64},{0,96},{33,1},{65,33},{97,65},{1,97},{34,2}... | collective-permute-start | bytes 786440 | tf_op jit(solution)/shard_map/ppermute | solution.py:20
  436.8 85.9 %collective-permute-start.22 = (f32[32,4,1,128]{3,2,1,0:T(1,128)S(1)}, f32[32,4,1,128]{3,2,1,0:T(1,128)S(1)}, u32[]{:S(2)}, u32[]{:S(2)}) collective-permute-start(f32[32,4,1,128]{3,2,1,0:T(1,128)S(1)} %get-tuple-element.2), channel_id=1, source_target_pairs={{0,1},{1,2},{2,3},{3,4},{4,5},{5,6},{6,7},{7,0},{8,9},{9,10},{10,1... | collective-permute-start | bytes 196616 | tf_op jit(solution)/shard_map/ppermute | solution.py:19
  478.9 43.8 %collective-permute-start.23 = (f32[32,4,1,128]{3,2,1,0:T(1,128)S(1)}, f32[32,4,1,128]{3,2,1,0:T(1,128)S(1)}, u32[]{:S(2)}, u32[]{:S(2)}) collective-permute-start(f32[32,4,1,128]{3,2,1,0:T(1,128)S(1)} %get-tuple-element.3), channel_id=1, source_target_pairs={{1,0},{2,1},{3,2},{4,3},{5,4},{6,5},{7,6},{0,7},{9,8},{10,9},{11,1... | collective-permute-start | bytes 196616 | tf_op jit(solution)/shard_map/ppermute | solution.py:20
  567.1 125.9 %all-gather.7.cloned.1.call-start = ((), (), s32[]{:S(2)}) async-start(), calls=%async_computation.1 | async-start | bytes 6291456 | tf_op jit(solution)/shard_map/all_gather | solution.py:40
Sparse Core Ops, SparseCore 0:
  567.2 59.7 all-gather.4
  631.0 61.8 all-gather.6
where the time goes:
time: 714 us; the launch traced here: 713 us
  waiting for transfers between devices  466 us (65%)
  other arithmetic  153 us (21%)
  local copies, waits for them, and re-layouts  42.4 us (6%)
  starting transfers between devices  37.7 us (5%)
  between operations  14.2 us (2%)
    ppermute x12, waiting for transfers between devices, padded_2(): lax.ppermute(last, axis, up)  222 us
    add x4, other arithmetic, march_step(): return middle + 0.1 * spread + 0.2 * middle * (1.0 - middle * crowding)  128 us
    all_gather x2, waiting for transfers between devices, prefix_by_axis(): pieces = lax.all_gather(so_far, axis)  122 us
    ppermute x12, waiting for transfers between devices, padded_2(): lax.ppermute(leading, axis, [(b, a) for a, b in up])  122 us
    ppermute x12, starting transfers between devices, padded_2(): lax.ppermute(leading, axis, [(b, a) for a, b in up])  29 us
    slice x11, local copies, waits for them, and re-layouts, padded_2(): last = lax.slice_in_dim(value, length - width, length, axis=dim)  19.8 us
  transfers between devices with their start and end apart: 26, of which 11 were waited for; matrix products, arithmetic and copies ran while one was open for 4% of the time, Pallas kernels for 0%

commit v1 on v0

v1 whole, which is shorter than its diff:
```python
import jax
import jax.numpy as jnp
from jax import lax
from jax.experimental import pallas as pl
from jax.experimental.pallas import tpu as pltpu
from jax.sharding import PartitionSpec as P

STEPS = 4
ROWS = 1
LAG = 2
AHEAD = 8
MESH = pl.DeviceIdType.MESH


def swap_kernel(
    sizes,
    d_hbm, c_hbm, run_hbm, end_hbm,
    even, odd, crowd, ghost, edge, there, below, totals, bases, run_own, run_there,
    z_send, z_recv, k_send, k_recv, p_send, p_recv, j_send, j_recv,
    in_send, in_recv, in_own, out_send, out_recv, base_send, base_recv,
    total_send, total_recv, write,
):
    n_lat, n_lon, n_lev, nj, ni, nk, cells = sizes
    half, blocks = nk // 2, nj // ROWS
    wide = 2 * ni
    a, b, m = lax.axis_index("lat"), lax.axis_index("lon"), lax.axis_index("lev")
    core, y_hi = lax.rem(a, 2), a // 2
    y_lo, z_hi = lax.rem(b, 2), b // 2
    h = lax.rem(y_lo + y_hi + m, 2)
    pair = b + 1 - 2 * y_lo
    peer_p = (a, pair, m)
    peer_z = (a, lax.rem(b + 2, n_lon), m)
    peer_k = (a, b, lax.rem(m + n_lev - 1 + 2 * h, n_lev))
    peer_c = (a + 1 - 2 * core, b, m)
    peer_j = (lax.rem(a + n_lat - 1 + 2 * core, n_lat), pair, m)
    states = (even, odd)

    barrier = pltpu.get_barrier_semaphore()
    peers = (peer_p, peer_z, peer_k, peer_c, peer_j)
    for peer in peers:
        pl.semaphore_signal(barrier, inc=1, device_id=peer, device_id_type=MESH)
    pl.semaphore_wait(barrier, len(peers))

    def first(block):
        return block * ROWS + (1 - core) * (nj - (2 * block + 1) * ROWS)

    def remote(src, dst, send, recv, peer):
        return pltpu.make_async_remote_copy(
            src_ref=src, dst_ref=dst, send_sem=send, recv_sem=recv,
            device_id=peer, device_id_type=MESH,
        )

    here = pl.ds(pl.multiple_of(half * h, 8), half)
    away = pl.ds(pl.multiple_of(half * (1 - h), 8), half)

    def bring_away(block):
        j = first(block)
        rows, padded = pl.ds(j, ROWS), pl.ds(j + 1, ROWS)
        mine, mine_in = pl.ds(1 + ni * y_lo, ni), pl.ds(ni * y_lo, ni)
        return (
            remote(d_hbm.at[rows, :, away], even.at[padded, mine], in_send.at[0, block], in_recv.at[0, block], peer_p),
            remote(c_hbm.at[rows, :, away], crowd.at[rows, mine_in], in_send.at[1, block], in_recv.at[1, block], peer_p),
        )

    def bring_own(block):
        j = first(block)
        rows, padded = pl.ds(j, ROWS), pl.ds(j + 1, ROWS)
        mine, mine_in = pl.ds(1 + ni * y_lo, ni), pl.ds(ni * y_lo, ni)
        return (
            pltpu.make_async_copy(d_hbm.at[rows, :, here], even.at[padded, mine], in_own.at[0, block]),
            pltpu.make_async_copy(c_hbm.at[rows, :, here], crowd.at[rows, mine_in], in_own.at[1, block]),
        )

    def start_bring(block):
        for copy in bring_away(block) + bring_own(block):
            copy.start()

    def wait_bring(block):
        for copy in bring_own(block):
            copy.wait()
        for copy in bring_away(block):
            copy.wait_recv()

    def face_copies(t, block):
        state, par, j = states[t % 2], t % 2, first(block)
        rows, padded = pl.ds(j, ROWS), pl.ds(j + 1, ROWS)
        return (
            remote(state.at[padded, 1], state.at[padded, wide + 1], z_send.at[par, 0, block], z_recv.at[par, 0, block], peer_z),
            remote(state.at[padded, wide], state.at[padded, 0], z_send.at[par, 1, block], z_recv.at[par, 1, block], peer_z),
            remote(edge.at[par, h, rows], ghost.at[par, 1 - h, rows], k_send.at[par, block], k_recv.at[par, block], peer_k),
            remote(edge.at[par, 1 - h, rows], ghost.at[par, h, rows], p_send.at[par, block], p_recv.at[par, block], peer_p),
        )

    def row_copy(t, side):
        state, par = states[t % 2], t % 2
        inner = pl.ds(1, wide)
        if side == 0:
            row, ring_row, peer = 1 + (1 - core) * (nj - 1), core * (nj + 1), peer_c
        else:
            row, ring_row, peer = 1 + core * (nj - 1), (1 - core) * (nj + 1), peer_j
        return remote(state.at[row, inner], state.at[ring_row, inner], j_send.at[par, side], j_recv.at[par, side], peer)

    def send_faces(t, block):
        for copy in face_copies(t, block):
            copy.start()

        @pl.when(block == 0)
        def _():
            row_copy(t, 0).start()

        @pl.when(block == blocks - 1)
        def _():
            row_copy(t, 1).start()

    def wait_faces(t, block):
        for copy in face_copies(t, block):
            copy.wait_recv()

        @pl.when(block == 0)
        def _():
            row_copy(t, 0).wait_recv()

        @pl.when(block == blocks - 1)
        def _():
            row_copy(t, 1).wait_recv()

    def sent_faces(t, block):
        for copy in face_copies(t, block):
            copy.wait_send()

        @pl.when(block == 0)
        def _():
            row_copy(t, 0).wait_send()

        @pl.when(block == blocks - 1)
        def _():
            row_copy(t, 1).wait_send()

    place = lax.broadcasted_iota(jnp.int32, (half, cells), 0)

    def arrive(block):
        wait_bring(block)
        for row in range(ROWS):
            j = first(block) + row
            for i in range(wide):
                edge[0, 0, j, i : i + 1, :] = even[j + 1, i + 1, 0:1, :]
                edge[0, 1, j, i : i + 1, :] = even[j + 1, i + 1, half - 1 : half, :]
        send_faces(0, block)

    def step(t, block):
        old, new, par = states[(t - 1) % 2], states[t % 2], (t - 1) % 2
        wait_faces(t - 1, block)
        if t >= 2:
            sent_faces(t - 2, block)
        for row in range(ROWS):
            j = first(block) + row
            r = j + 1
            lower, middle = old[r, 0], old[r, 1]
            for i in range(wide):
                upper = old[r, i + 2]
                low = jnp.where(place == 0, ghost[par, 0, j, i : i + 1, :], pltpu.roll(middle, 1, 0))
                high = jnp.where(place == half - 1, ghost[par, 1, j, i : i + 1, :], pltpu.roll(middle, half - 1, 0))
                around = (lower + upper) + (old[r - 1, i + 1] + old[r + 1, i + 1]) + (low + high)
                value = 0.1 * around + middle * (0.6 - 0.2 * (crowd[j, i] * middle))
                new[r, i + 1] = value
                if t < STEPS:
                    edge[t % 2, 0, j, i : i + 1, :] = value[0:1]
                    edge[t % 2, 1, j, i : i + 1, :] = value[half - 1 : half]
                lower, middle = middle, upper
        if t < STEPS:
            send_faces(t, block)

    final = states[STEPS % 2]

    def out_copy(block):
        j = first(block)
        theirs = pl.ds(1 + ni * (1 - y_lo), ni)
        return remote(final.at[pl.ds(j + 1, ROWS), theirs], there.at[pl.ds(j, ROWS)], out_send.at[block], out_recv.at[block], peer_p)

    def own_copy(block):
        j = first(block)
        mine = pl.ds(1 + ni * y_lo, ni)
        return pltpu.make_async_copy(final.at[pl.ds(j + 1, ROWS), mine], end_hbm.at[pl.ds(j, ROWS), :, here], write.at[0, block])

    def total_copy(block):
        rows = pl.ds(first(block), ROWS)
        return remote(totals.at[rows], below.at[rows], total_send.at[block], total_recv.at[block], peer_z)

    def base_copy(block):
        rows = pl.ds(first(block), ROWS)
        return remote(bases.at[0, rows], bases.at[1, rows], base_send.at[block], base_recv.at[block], peer_p)

    def run_own_copy(block):
        rows = pl.ds(first(block), ROWS)
        return pltpu.make_async_copy(run_own.at[rows], run_hbm.at[rows, :, here], write.at[1, block])

    def there_copies(block):
        rows = pl.ds(first(block), ROWS)
        return (
            pltpu.make_async_copy(there.at[rows], end_hbm.at[rows, :, away], write.at[2, block]),
            pltpu.make_async_copy(run_there.at[rows], run_hbm.at[rows, :, away], write.at[3, block]),
        )

    def finish(block):
        out_copy(block).start()
        own_copy(block).start()

        @pl.when(z_hi == 0)
        def _():
            for row in range(ROWS):
                j = first(block) + row
                total = final[j + 1, 1]
                for i in range(1, wide):
                    total = total + final[j + 1, i + 1]
                totals[j] = total
                below[j] = jnp.zeros_like(total)
            total_copy(block).start()

    def sums(block):
        @pl.when(z_hi == 1)
        def _():
            total_copy(block).wait_recv()

        sent_faces(STEPS - 1, block)
        for row in range(ROWS):
            j = first(block) + row
            base = below[j]
            lowest = final[j + 1, 1]
            for i in range(1, ni):
                lowest = lowest + final[j + 1, i + 1]
            bases[0, j] = base + jnp.where(y_lo == 0, lowest, 0.0)
            run = base + jnp.where(y_lo == 1, lowest, 0.0)
            for i in range(ni):
                run = run + final[j + 1, 1 + ni * y_lo + i]
                run_own[j, i] = run * (1.0 / (ni * n_lon))
        base_copy(block).start()
        run_own_copy(block).start()

    def returned(block):
        out_copy(block).wait_recv()
        base_copy(block).wait_recv()
        for row in range(ROWS):
            j = first(block) + row
            run = bases[1, j]
            for i in range(ni):
                run = run + there[j, i]
                run_there[j, i] = run * (1.0 / (ni * n_lon))
        for copy in there_copies(block):
            copy.start()

    def guarded(stage, block):
        @pl.when((block >= 0) & (block < blocks))
        def _():
            stage(block)

    def close(block):
        for copy in bring_away(block):
            copy.wait_send()
        out_copy(block).wait_send()
        base_copy(block).wait_send()

        @pl.when(z_hi == 0)
        def _():
            total_copy(block).wait_send()

        own_copy(block).wait()
        run_own_copy(block).wait()
        for copy in there_copies(block):
            copy.wait()

    lax.fori_loop(0, min(AHEAD, blocks), lambda n, _: (start_bring(n), 0)[1], 0)

    def tick(n, carry):
        @pl.when(n + AHEAD < blocks)
        def _():
            start_bring(n + AHEAD)

        guarded(returned, n - LAG * (STEPS + 2))
        guarded(sums, n - LAG * (STEPS + 1))

        def last(block):
            step(STEPS, block)
            finish(block)

        guarded(last, n - LAG * STEPS)
        for t in range(STEPS - 1, 0, -1):
            guarded(lambda block, t=t: step(t, block), n - LAG * t)
        guarded(arrive, n)
        return carry

    lax.fori_loop(0, blocks + LAG * (STEPS + 2), tick, 0)
    lax.fori_loop(0, blocks, lambda n, _: (close(n), 0)[1], 0)


def solution(mesh):
    n_lat, n_lon, n_lev = (mesh.shape[axis] for axis in ("lat", "lon", "lev"))

    def body(density, crowding):
        nj, ni, nk, cells = density.shape
        half, blocks, wide = nk // 2, nj // ROWS, 2 * ni
        f32, dma = jnp.float32, pltpu.SemaphoreType.DMA
        out = jax.ShapeDtypeStruct(density.shape, f32)
        vmem = [
            (nj + 2, wide + 2, half, cells),
            (nj + 2, wide + 2, half, cells),
            (nj, wide, half, cells),
            (2, 2, nj, wide, cells),
            (2, 2, nj, wide, cells),
            (nj, ni, half, cells),
            (nj, half, cells),
            (nj, half, cells),
            (2, nj, half, cells),
            (nj, ni, half, cells),
            (nj, ni, half, cells),
        ]
        sems = [
            (2, 2, blocks), (2, 2, blocks), (2, blocks), (2, blocks), (2, blocks), (2, blocks), (2, 2), (2, 2),
            (2, blocks), (2, blocks), (2, blocks), (blocks,), (blocks,), (blocks,), (blocks,),
            (blocks,), (blocks,), (4, blocks),
        ]
        sizes = (n_lat, n_lon, n_lev, nj, ni, nk, cells)
        anywhere = pl.BlockSpec(memory_space=pl.ANY)

        def kernel(*refs):
            swap_kernel(sizes, *refs)

        return pl.pallas_call(
            kernel,
            out_shape=(out, out),
            in_specs=[anywhere, anywhere],
            out_specs=(anywhere, anywhere),
            scratch_shapes=[pltpu.VMEM(shape, f32) for shape in vmem] + [dma(shape) for shape in sems],
            compiler_params=pltpu.CompilerParams(
                collective_id=0, has_side_effects=True, vmem_limit_bytes=67043328
            ),
            cost_estimate=pl.CostEstimate(flops=14 * STEPS * density.size, bytes_accessed=16 * density.size, transcendentals=0),
            name="swap_sweep",
        )(density, crowding)

    spec = P("lat", "lon", "lev", None)
    return jax.shard_map(body, mesh=mesh, in_specs=(spec, spec), out_specs=(spec, spec), check_vma=False)
```

time: 714 us -> 350 us (0.49)
  waiting for transfers between devices: 466 us -> 0 us
  Pallas kernels: 0 us -> 335 us
  other arithmetic: 153 us -> 0 us
  starting transfers between devices: 37.7 us -> 0 us
  local copies, waits for them, and re-layouts: 42.4 us -> 11.4 us
  between operations: 14.2 us -> 0.65 us
    ppermute x24 -> x0, waiting for transfers between devices: 344 us -> none  [the longest x12 222 us: padded_2(): lax.ppermute(last, axis, up)]
    pallas_call x0 -> x1, Pallas kernels: none -> 335 us  [body(): pl.pallas_call(kernel, out_shape=(out, out), in_specs=[anywhere, anywhere...]
    add x6 -> x0, other arithmetic: 136 us -> none  [the longest x4 128 us: march_step(): return middle + 0.1 * spread + 0.2 * middle * (1.0 - middle * crowding)]
    all_gather x2 -> x0, waiting for transfers between devices: 122 us -> none  [prefix_by_axis(): pieces = lax.all_gather(so_far, axis)]
    ppermute x24 -> x0, starting transfers between devices: 37.7 us -> none  [the longest x12 29 us: padded_2(): lax.ppermute(leading, axis, [(b, a) for a, b in up])]
    slice x13 -> x0, local copies, waits for them, and re-layouts: 23 us -> none  [the longest x11 19.8 us: padded_2(): last = lax.slice_in_dim(value, length - width, length, axis=dim)]
    pad x8 -> x0, local copies, waits for them, and re-layouts: 13.1 us -> none  [the longest x4 6.6 us: padded_2(): jnp.pad(low, around)]
    div x1 -> x0, other arithmetic: 8.71 us -> none  [body(): running_total = (here + below) / (density.shape[1] * lax.axis_size(LON))]
  transfers between devices with their start and end apart: 26 -> 0, of which waited for: 11 -> 0; matrix products, arithmetic and copies ran while one was open for 4% -> 0% of each run, Pallas kernels for 0% -> 0%
where the time goes in v1:
time: 350 us; the launch traced here: 347 us
  Pallas kernels  335 us (96%)
  local copies, waits for them, and re-layouts  11.4 us (3%)
    pallas_call x1, Pallas kernels, body(): pl.pallas_call(kernel, out_shape=(out, out), in_specs=[anywhere, anywhere...  335 us
    unnamed x4, local copies, waits for them, and re-layouts  11.4 us

profile of v1, /device:TPU:0, one launch (start us, length us, event | category | flops | bytes accessed | tf_op | source)
XLA Modules:
  0.0 346.8 jit_solution(16403162414810476471)
XLA Ops:
  0.6 334.8 %swap_sweep.1 = (f32[32,4,128,128]{3,2,1,0:T(8,128)}, f32[32,4,128,128]{3,2,1,0:T(8,128)}) custom-call(f32[32,4,128,128]{3,2,1,0:T(8,128)} %refs_0_.1, f32[32,4,128,128]{3,2,1,0:T(8,128)} %refs_1_.1), custom_call_target="tpu_custom_call" | custom-call | flops 117440512 | bytes 33554432 | tf_op jit(solution)/shard_map/swap_sweep/pallas_call | solution.py:327
  335.4 0.0 copy-start
  335.4 8.0 %copy.6 = f32[32,4,128,128]{3,2,1,0:T(8,128)} copy(f32[32,4,128,128]{3,2,1,0:T(8,128)} %get-tuple-element.4) | data formatting | bytes 16777216
  343.4 0.0 copy-done
  343.4 3.4 copy.7
Async XLA Ops:
  335.4 8.1 %copy-start = (f32[32,4,128,128]{3,2,1,0:T(8,128)S(1)}, f32[32,4,128,128]{3,2,1,0:T(8,128)}, u32[]{:S(2)}) copy-start(f32[32,4,128,128]{3,2,1,0:T(8,128)} %get-tuple-element.5) | copy-start | bytes 25165828

commit v2 on v1

--- a/solution.py
+++ b/solution.py
@@ -7,18 +7,19 @@
 
 STEPS = 4
 ROWS = 1
-LAG = 2
-AHEAD = 8
+LAG = 3
+AHEAD = 2
+PIECES = 4
 MESH = pl.DeviceIdType.MESH
 
 
 def swap_kernel(
     sizes,
-    d_hbm, c_hbm, run_hbm, end_hbm,
-    even, odd, crowd, ghost, edge, there, below, totals, bases, run_own, run_there,
+    d_hbm, c_hbm, run_out, end_out,
+    even, odd, crowd, ghost, edge, below, totals, bases,
     z_send, z_recv, k_send, k_recv, p_send, p_recv, j_send, j_recv,
     in_send, in_recv, in_own, out_send, out_recv, base_send, base_recv,
-    total_send, total_recv, write,
+    total_send, total_recv,
 ):
     n_lat, n_lon, n_lev, nj, ni, nk, cells = sizes
     half, blocks = nk // 2, nj // ROWS
@@ -175,12 +176,7 @@
     def out_copy(block):
         j = first(block)
         theirs = pl.ds(1 + ni * (1 - y_lo), ni)
-        return remote(final.at[pl.ds(j + 1, ROWS), theirs], there.at[pl.ds(j, ROWS)], out_send.at[block], out_recv.at[block], peer_p)
-
-    def own_copy(block):
-        j = first(block)
-        mine = pl.ds(1 + ni * y_lo, ni)
-        return pltpu.make_async_copy(final.at[pl.ds(j + 1, ROWS), mine], end_hbm.at[pl.ds(j, ROWS), :, here], write.at[0, block])
+        return remote(final.at[pl.ds(j + 1, ROWS), theirs], end_out.at[pl.ds(j, ROWS), :, here], out_send.at[block], out_recv.at[block], peer_p)
 
     def total_copy(block):
         rows = pl.ds(first(block), ROWS)
@@ -190,20 +186,8 @@
         rows = pl.ds(first(block), ROWS)
         return remote(bases.at[0, rows], bases.at[1, rows], base_send.at[block], base_recv.at[block], peer_p)
 
-    def run_own_copy(block):
-        rows = pl.ds(first(block), ROWS)
-        return pltpu.make_async_copy(run_own.at[rows], run_hbm.at[rows, :, here], write.at[1, block])
-
-    def there_copies(block):
-        rows = pl.ds(first(block), ROWS)
-        return (
-            pltpu.make_async_copy(there.at[rows], end_hbm.at[rows, :, away], write.at[2, block]),
-            pltpu.make_async_copy(run_there.at[rows], run_hbm.at[rows, :, away], write.at[3, block]),
-        )
-
     def finish(block):
         out_copy(block).start()
-        own_copy(block).start()
 
         @pl.when(z_hi == 0)
         def _():
@@ -231,10 +215,11 @@
             bases[0, j] = base + jnp.where(y_lo == 0, lowest, 0.0)
             run = base + jnp.where(y_lo == 1, lowest, 0.0)
             for i in range(ni):
-                run = run + final[j + 1, 1 + ni * y_lo + i]
-                run_own[j, i] = run * (1.0 / (ni * n_lon))
+                value = final[j + 1, 1 + ni * y_lo + i]
+                end_out[j, i, here] = value
+                run = run + value
+                run_out[j, i, here] = run * (1.0 / (ni * n_lon))
         base_copy(block).start()
-        run_own_copy(block).start()
 
     def returned(block):
         out_copy(block).wait_recv()
@@ -243,10 +228,8 @@
             j = first(block) + row
             run = bases[1, j]
             for i in range(ni):
-                run = run + there[j, i]
-                run_there[j, i] = run * (1.0 / (ni * n_lon))
-        for copy in there_copies(block):
-            copy.start()
+                run = run + end_out[j, i, away]
+                run_out[j, i, away] = run * (1.0 / (ni * n_lon))
 
     def guarded(stage, block):
         @pl.when((block >= 0) & (block < blocks))
@@ -263,11 +246,6 @@
         def _():
             total_copy(block).wait_send()
 
-        own_copy(block).wait()
-        run_own_copy(block).wait()
-        for copy in there_copies(block):
-            copy.wait()
-
     lax.fori_loop(0, min(AHEAD, blocks), lambda n, _: (start_bring(n), 0)[1], 0)
 
     def tick(n, carry):
@@ -292,6 +270,19 @@
     lax.fori_loop(0, blocks, lambda n, _: (close(n), 0)[1], 0)
 
 
+def flush_kernel(run_in, end_in, run_out, end_out, sems):
+    copies = []
+    for k in range(PIECES):
+        size = run_in.shape[0] // PIECES
+        rows = pl.ds(k * size, size)
+        copies.append(pltpu.make_async_copy(run_in.at[rows], run_out.at[rows], sems.at[0, k]))
+        copies.append(pltpu.make_async_copy(end_in.at[rows], end_out.at[rows], sems.at[1, k]))
+    for copy in copies:
+        copy.start()
+    for copy in copies:
+        copy.wait()
+
+
 def solution(mesh):
     n_lat, n_lon, n_lev = (mesh.shape[axis] for axis in ("lat", "lon", "lev"))
 
@@ -299,43 +290,52 @@
         nj, ni, nk, cells = density.shape
         half, blocks, wide = nk // 2, nj // ROWS, 2 * ni
         f32, dma = jnp.float32, pltpu.SemaphoreType.DMA
-        out = jax.ShapeDtypeStruct(density.shape, f32)
+        out = pltpu.VMEM(density.shape, f32)
         vmem = [
             (nj + 2, wide + 2, half, cells),
             (nj + 2, wide + 2, half, cells),
             (nj, wide, half, cells),
             (2, 2, nj, wide, cells),
             (2, 2, nj, wide, cells),
-            (nj, ni, half, cells),
             (nj, half, cells),
             (nj, half, cells),
             (2, nj, half, cells),
-            (nj, ni, half, cells),
-            (nj, ni, half, cells),
         ]
         sems = [
             (2, 2, blocks), (2, 2, blocks), (2, blocks), (2, blocks), (2, blocks), (2, blocks), (2, 2), (2, 2),
             (2, blocks), (2, blocks), (2, blocks), (blocks,), (blocks,), (blocks,), (blocks,),
-            (blocks,), (blocks,), (4, blocks),
+            (blocks,), (blocks,),
         ]
         sizes = (n_lat, n_lon, n_lev, nj, ni, nk, cells)
         anywhere = pl.BlockSpec(memory_space=pl.ANY)
+        inside = pl.BlockSpec(memory_space=pltpu.VMEM)
 
         def kernel(*refs):
             swap_kernel(sizes, *refs)
 
-        return pl.pallas_call(
+        results = pl.pallas_call(
             kernel,
             out_shape=(out, out),
             in_specs=[anywhere, anywhere],
-            out_specs=(anywhere, anywhere),
+            out_specs=(inside, inside),
             scratch_shapes=[pltpu.VMEM(shape, f32) for shape in vmem] + [dma(shape) for shape in sems],
             compiler_params=pltpu.CompilerParams(
-                collective_id=0, has_side_effects=True, vmem_limit_bytes=67043328
+                collective_id=0, has_side_effects=True, vmem_limit_bytes=48 * 1024 * 1024 - 8 * 1024 * 128
             ),
             cost_estimate=pl.CostEstimate(flops=14 * STEPS * density.size, bytes_accessed=16 * density.size, transcendentals=0),
             name="swap_sweep",
         )(density, crowding)
+        whole = jax.ShapeDtypeStruct(density.shape, f32)
+        return pl.pallas_call(
+            flush_kernel,
+            out_shape=(whole, whole),
+            in_specs=[inside, inside],
+            out_specs=(anywhere, anywhere),
+            scratch_shapes=[dma((2, PIECES))],
+            compiler_params=pltpu.CompilerParams(vmem_limit_bytes=1024 * 1024),
+            cost_estimate=pl.CostEstimate(flops=density.size, bytes_accessed=16 * density.size, transcendentals=0),
+            name="flush",
+        )(*results)
 
     spec = P("lat", "lon", "lev", None)
     return jax.shard_map(body, mesh=mesh, in_specs=(spec, spec), out_specs=(spec, spec), check_vma=False)

time: 350 us -> 325 us (0.929)
  local copies, waits for them, and re-layouts: 11.4 us -> 0 us
  Pallas kernels: 335 us -> 324 us
    pallas_call x1, Pallas kernels: 335 us -> 318 us  [body(): pl.pallas_call(kernel, out_shape=(out, out), in_specs=[anywhere, anywhere...]
    unnamed x4 -> x0, local copies, waits for them, and re-layouts: 11.4 us -> none
    pallas_call x0 -> x1, Pallas kernels: none -> 5.92 us  [body(): pl.pallas_call(flush_kernel, out_shape=(whole, whole), in_specs=[inside,...]
where the time goes in v2:
time: 325 us
  Pallas kernels  324 us (100%)
    pallas_call x1, Pallas kernels, body(): pl.pallas_call(kernel, out_shape=(out, out), in_specs=[anywhere, anywhere...  318 us

profile of v2, /device:TPU:0, one launch (start us, length us, event | category | flops | bytes accessed | tf_op | source)
XLA Modules:
  0.0 324.8 jit_solution(11577280980551199944)
XLA Ops:
  0.6 318.2 %swap_sweep.1 = (f32[32,4,128,128]{3,2,1,0:T(8,128)S(1)}, f32[32,4,128,128]{3,2,1,0:T(8,128)S(1)}) custom-call(f32[32,4,128,128]{3,2,1,0:T(8,128)} %refs_0_.1, f32[32,4,128,128]{3,2,1,0:T(8,128)} %refs_1_.1), custom_call_target="tpu_custom_call" | custom-call | flops 117440512 | bytes 33554432 | tf_op jit(solution)/shard_map/swap_sweep/pallas_call | solution.py:316
  318.9 5.9 %flush.1 = (f32[32,4,128,128]{3,2,1,0:T(8,128)}, f32[32,4,128,128]{3,2,1,0:T(8,128)}) custom-call(f32[32,4,128,128]{3,2,1,0:T(8,128)S(1)} %get-tuple-element.4.run_in, f32[32,4,128,128]{3,2,1,0:T(8,128)S(1)} %get-tuple-element.5.end_in), custom_call_target="tpu_custom_call" | custom-call | flops 2097152 | bytes 33554432 | tf_op jit(solution)/shard_map/flush/pallas_call | solution.py:329

commit v3 on v2

--- a/solution.py
+++ b/solution.py
@@ -8,8 +8,10 @@
 STEPS = 4
 ROWS = 1
 LAG = 3
-AHEAD = 2
+LAST = 2
+AHEAD = 1
 PIECES = 4
+LOADS = 4
 MESH = pl.DeviceIdType.MESH
 
 
@@ -17,7 +19,7 @@
     sizes,
     d_hbm, c_hbm, run_out, end_out,
     even, odd, crowd, ghost, edge, below, totals, bases,
-    z_send, z_recv, k_send, k_recv, p_send, p_recv, j_send, j_recv,
+    z_send, z_recv, k_send, k_recv, j_send, j_recv,
     in_send, in_recv, in_own, out_send, out_recv, base_send, base_recv,
     total_send, total_recv,
 ):
@@ -27,20 +29,19 @@
     a, b, m = lax.axis_index("lat"), lax.axis_index("lon"), lax.axis_index("lev")
     core, y_hi = lax.rem(a, 2), a // 2
     y_lo, z_hi = lax.rem(b, 2), b // 2
-    h = lax.rem(y_lo + y_hi + m, 2)
+    h = lax.rem(y_lo + y_hi, 2)
     pair = b + 1 - 2 * y_lo
     peer_p = (a, pair, m)
     peer_z = (a, lax.rem(b + 2, n_lon), m)
-    peer_k = (a, b, lax.rem(m + n_lev - 1 + 2 * h, n_lev))
+    peer_k = ((a, b, lax.rem(m + n_lev - 1, n_lev)), (a, b, lax.rem(m + 1, n_lev)))
     peer_c = (a + 1 - 2 * core, b, m)
     peer_j = (lax.rem(a + n_lat - 1 + 2 * core, n_lat), pair, m)
     states = (even, odd)
 
     barrier = pltpu.get_barrier_semaphore()
-    peers = (peer_p, peer_z, peer_k, peer_c, peer_j)
+    peers = (peer_p, peer_z, *peer_k, peer_c, peer_j)
     for peer in peers:
         pl.semaphore_signal(barrier, inc=1, device_id=peer, device_id_type=MESH)
-    pl.semaphore_wait(barrier, len(peers))
 
     def first(block):
         return block * ROWS + (1 - core) * (nj - (2 * block + 1) * ROWS)
@@ -53,34 +54,51 @@
 
     here = pl.ds(pl.multiple_of(half * h, 8), half)
     away = pl.ds(pl.multiple_of(half * (1 - h), 8), half)
-
-    def bring_away(block):
+    lane = lax.broadcasted_iota(jnp.int32, (half, cells), 1)
+    mine = jnp.where(lane >= cells // 2, 1, 0) == h
+    place = lax.broadcasted_iota(jnp.int32, (half, cells), 0)
+    left = lax.broadcasted_iota(jnp.int32, (wide, cells), 1) < cells // 2
+
+    def swing(value):
+        return pltpu.roll(value, cells // 2, 1)
+
+    def load(block):
+        rows = pl.ds(first(block), ROWS)
+        return (
+            pltpu.make_async_copy(d_hbm.at[rows], end_out.at[rows], in_own.at[0, block]),
+            pltpu.make_async_copy(c_hbm.at[rows], run_out.at[rows], in_own.at[1, block]),
+        )
+
+    def start_load(block):
+        for copy in load(block):
+            copy.start()
+
+    def pack(block):
+        for copy in load(block):
+            copy.wait()
+        for row in range(ROWS):
+            j = first(block) + row
+            for q in range(ni):
+                for source, kept in (
+                    (end_out, even.at[j + 1, 1 + ni * y_lo + q]),
+                    (run_out, crowd.at[j, ni * y_lo + q]),
+                ):
+                    near, far = source[j, q, here], source[j, q, away]
+                    kept[...] = jnp.where(mine, near, swing(far))
+                    source[j, q, 0:half] = jnp.where(mine, swing(near), far)
+
+    def give(block):
         j = first(block)
         rows, padded = pl.ds(j, ROWS), pl.ds(j + 1, ROWS)
-        mine, mine_in = pl.ds(1 + ni * y_lo, ni), pl.ds(ni * y_lo, ni)
+        packed = pl.ds(0, half)
         return (
-            remote(d_hbm.at[rows, :, away], even.at[padded, mine], in_send.at[0, block], in_recv.at[0, block], peer_p),
-            remote(c_hbm.at[rows, :, away], crowd.at[rows, mine_in], in_send.at[1, block], in_recv.at[1, block], peer_p),
+            remote(end_out.at[rows, :, packed], even.at[padded, pl.ds(1 + ni * y_lo, ni)], in_send.at[0, block], in_recv.at[0, block], peer_p),
+            remote(run_out.at[rows, :, packed], crowd.at[rows, pl.ds(ni * y_lo, ni)], in_send.at[1, block], in_recv.at[1, block], peer_p),
         )
 
-    def bring_own(block):
-        j = first(block)
-        rows, padded = pl.ds(j, ROWS), pl.ds(j + 1, ROWS)
-        mine, mine_in = pl.ds(1 + ni * y_lo, ni), pl.ds(ni * y_lo, ni)
-        return (
-            pltpu.make_async_copy(d_hbm.at[rows, :, here], even.at[padded, mine], in_own.at[0, block]),
-            pltpu.make_async_copy(c_hbm.at[rows, :, here], crowd.at[rows, mine_in], in_own.at[1, block]),
-        )
-
-    def start_bring(block):
-        for copy in bring_away(block) + bring_own(block):
+    def start_give(block):
+        for copy in give(block):
             copy.start()
-
-    def wait_bring(block):
-        for copy in bring_own(block):
-            copy.wait()
-        for copy in bring_away(block):
-            copy.wait_recv()
 
     def face_copies(t, block):
         state, par, j = states[t % 2], t % 2, first(block)
@@ -88,8 +106,8 @@
         return (
             remote(state.at[padded, 1], state.at[padded, wide + 1], z_send.at[par, 0, block], z_recv.at[par, 0, block], peer_z),
             remote(state.at[padded, wide], state.at[padded, 0], z_send.at[par, 1, block], z_recv.at[par, 1, block], peer_z),
-            remote(edge.at[par, h, rows], ghost.at[par, 1 - h, rows], k_send.at[par, block], k_recv.at[par, block], peer_k),
-            remote(edge.at[par, 1 - h, rows], ghost.at[par, h, rows], p_send.at[par, block], p_recv.at[par, block], peer_p),
+            remote(edge.at[par, 0, rows], ghost.at[par, 1, rows], k_send.at[par, 0, block], k_recv.at[par, 0, block], peer_k[0]),
+            remote(edge.at[par, 1, rows], ghost.at[par, 0, rows], k_send.at[par, 1, block], k_recv.at[par, 1, block], peer_k[1]),
         )
 
     def row_copy(t, side):
@@ -137,10 +155,9 @@
         def _():
             row_copy(t, 1).wait_send()
 
-    place = lax.broadcasted_iota(jnp.int32, (half, cells), 0)
-
     def arrive(block):
-        wait_bring(block)
+        for copy in give(block):
+            copy.wait_recv()
         for row in range(ROWS):
             j = first(block) + row
             for i in range(wide):
@@ -156,11 +173,13 @@
         for row in range(ROWS):
             j = first(block) + row
             r = j + 1
+            ends = swing(jnp.where(left, edge[par, 1, j], ghost[par, 0, j]))
+            starts = swing(jnp.where(left, ghost[par, 1, j], edge[par, 0, j]))
             lower, middle = old[r, 0], old[r, 1]
             for i in range(wide):
                 upper = old[r, i + 2]
-                low = jnp.where(place == 0, ghost[par, 0, j, i : i + 1, :], pltpu.roll(middle, 1, 0))
-                high = jnp.where(place == half - 1, ghost[par, 1, j, i : i + 1, :], pltpu.roll(middle, half - 1, 0))
+                low = jnp.where(place == 0, ends[i : i + 1], pltpu.roll(middle, 1, 0))
+                high = jnp.where(place == half - 1, starts[i : i + 1], pltpu.roll(middle, half - 1, 0))
                 around = (lower + upper) + (old[r - 1, i + 1] + old[r + 1, i + 1]) + (low + high)
                 value = 0.1 * around + middle * (0.6 - 0.2 * (crowd[j, i] * middle))
                 new[r, i + 1] = value
@@ -176,7 +195,7 @@
     def out_copy(block):
         j = first(block)
         theirs = pl.ds(1 + ni * (1 - y_lo), ni)
-        return remote(final.at[pl.ds(j + 1, ROWS), theirs], end_out.at[pl.ds(j, ROWS), :, here], out_send.at[block], out_recv.at[block], peer_p)
+        return remote(final.at[pl.ds(j + 1, ROWS), theirs], end_out.at[pl.ds(j, ROWS), :, pl.ds(half, half)], out_send.at[block], out_recv.at[block], peer_p)
 
     def total_copy(block):
         rows = pl.ds(first(block), ROWS)
@@ -213,23 +232,26 @@
             for i in range(1, ni):
                 lowest = lowest + final[j + 1, i + 1]
             bases[0, j] = base + jnp.where(y_lo == 0, lowest, 0.0)
-            run = base + jnp.where(y_lo == 1, lowest, 0.0)
-            for i in range(ni):
-                value = final[j + 1, 1 + ni * y_lo + i]
-                end_out[j, i, here] = value
-                run = run + value
-                run_out[j, i, here] = run * (1.0 / (ni * n_lon))
+            bases[2, j] = base + jnp.where(y_lo == 1, lowest, 0.0)
         base_copy(block).start()
 
     def returned(block):
         out_copy(block).wait_recv()
         base_copy(block).wait_recv()
-        for row in range(ROWS):
-            j = first(block) + row
-            run = bases[1, j]
-            for i in range(ni):
-                run = run + end_out[j, i, away]
-                run_out[j, i, away] = run * (1.0 / (ni * n_lon))
+        for copy in give(block):
+            copy.wait_send()
+        scale = 1.0 / (ni * n_lon)
+        for row in range(ROWS):
+            j = first(block) + row
+            run, run_pair = bases[2, j], bases[1, j]
+            for q in range(ni):
+                value, value_pair = final[j + 1, 1 + ni * y_lo + q], end_out[j, q, half:nk]
+                run, run_pair = run + value, run_pair + value_pair
+                end_out[j, q, here] = jnp.where(mine, value, swing(value_pair))
+                end_out[j, q, away] = jnp.where(mine, swing(value), value_pair)
+                scaled, scaled_pair = run * scale, run_pair * scale
+                run_out[j, q, here] = jnp.where(mine, scaled, swing(scaled_pair))
+                run_out[j, q, away] = jnp.where(mine, swing(scaled), scaled_pair)
 
     def guarded(stage, block):
         @pl.when((block >= 0) & (block < blocks))
@@ -237,8 +259,6 @@
             stage(block)
 
     def close(block):
-        for copy in bring_away(block):
-            copy.wait_send()
         out_copy(block).wait_send()
         base_copy(block).wait_send()
 
@@ -246,15 +266,21 @@
         def _():
             total_copy(block).wait_send()
 
-    lax.fori_loop(0, min(AHEAD, blocks), lambda n, _: (start_bring(n), 0)[1], 0)
+    def prepare(n, carry):
+        guarded(start_give, n)
+        guarded(start_load, n + LOADS)
+        guarded(pack, n + 1)
+        return carry
+
+    lax.fori_loop(0, LOADS, lambda n, carry: (start_load(n), carry)[1], 0)
+    pack(0)
+    pl.semaphore_wait(barrier, len(peers))
+    lax.fori_loop(0, AHEAD, prepare, 0)
 
     def tick(n, carry):
-        @pl.when(n + AHEAD < blocks)
-        def _():
-            start_bring(n + AHEAD)
-
-        guarded(returned, n - LAG * (STEPS + 2))
-        guarded(sums, n - LAG * (STEPS + 1))
+        prepare(n + AHEAD, 0)
+        guarded(returned, n - LAG * STEPS - 2 * LAST)
+        guarded(sums, n - LAG * STEPS - LAST)
 
         def last(block):
             step(STEPS, block)
@@ -266,7 +292,7 @@
         guarded(arrive, n)
         return carry
 
-    lax.fori_loop(0, blocks + LAG * (STEPS + 2), tick, 0)
+    lax.fori_loop(0, blocks + LAG * STEPS + 2 * LAST, tick, 0)
     lax.fori_loop(0, blocks, lambda n, _: (close(n), 0)[1], 0)
 
 
@@ -299,10 +325,10 @@
             (2, 2, nj, wide, cells),
             (nj, half, cells),
             (nj, half, cells),
-            (2, nj, half, cells),
+            (3, nj, half, cells),
         ]
         sems = [
-            (2, 2, blocks), (2, 2, blocks), (2, blocks), (2, blocks), (2, blocks), (2, blocks), (2, 2), (2, 2),
+            (2, 2, blocks), (2, 2, blocks), (2, 2, blocks), (2, 2, blocks), (2, 2), (2, 2),
             (2, blocks), (2, blocks), (2, blocks), (blocks,), (blocks,), (blocks,), (blocks,),
             (blocks,), (blocks,),
         ]
@@ -320,7 +346,7 @@
             out_specs=(inside, inside),
             scratch_shapes=[pltpu.VMEM(shape, f32) for shape in vmem] + [dma(shape) for shape in sems],
             compiler_params=pltpu.CompilerParams(
-                collective_id=0, has_side_effects=True, vmem_limit_bytes=48 * 1024 * 1024 - 8 * 1024 * 128
+                collective_id=0, has_side_effects=True, vmem_limit_bytes=47 * 1024 * 1024
             ),
             cost_estimate=pl.CostEstimate(flops=14 * STEPS * density.size, bytes_accessed=16 * density.size, transcendentals=0),
             name="swap_sweep",

time: 325 us -> 314 us (0.966)
  Pallas kernels: 324 us -> 313 us
    pallas_call x1, Pallas kernels: 318 us -> 307 us  [body(): pl.pallas_call(kernel, out_shape=(out, out), in_specs=[anywhere, anywhere...]
where the time goes in v3:
time: 314 us
  Pallas kernels  313 us (100%)
    pallas_call x1, Pallas kernels, body(): pl.pallas_call(kernel, out_shape=(out, out), in_specs=[anywhere, anywhere...  307 us

profile of v3, /device:TPU:0, one launch (start us, length us, event | category | flops | bytes accessed | tf_op | source)
XLA Modules:
  0.0 313.9 jit_solution(14838104621602785399)
XLA Ops:
  0.6 307.4 %swap_sweep.1 = (f32[32,4,128,128]{3,2,1,0:T(8,128)S(1)}, f32[32,4,128,128]{3,2,1,0:T(8,128)S(1)}) custom-call(f32[32,4,128,128]{3,2,1,0:T(8,128)} %refs_0_.1, f32[32,4,128,128]{3,2,1,0:T(8,128)} %refs_1_.1), custom_call_target="tpu_custom_call" | custom-call | flops 117440512 | bytes 33554432 | tf_op jit(solution)/shard_map/swap_sweep/pallas_call | solution.py:342
  308.0 5.9 %flush.1 = (f32[32,4,128,128]{3,2,1,0:T(8,128)}, f32[32,4,128,128]{3,2,1,0:T(8,128)}) custom-call(f32[32,4,128,128]{3,2,1,0:T(8,128)S(1)} %get-tuple-element.4.run_in, f32[32,4,128,128]{3,2,1,0:T(8,128)S(1)} %get-tuple-element.5.end_in), custom_call_target="tpu_custom_call" | custom-call | flops 2097152 | bytes 33554432 | tf_op jit(solution)/shard_map/flush/pallas_call | solution.py:355

commit v4 on v3

--- a/solution.py
+++ b/solution.py
@@ -6,9 +6,11 @@
 from jax.sharding import PartitionSpec as P
 
 STEPS = 4
-ROWS = 1
-LAG = 3
-LAST = 2
+ROWS = 2
+LAG = 2
+LAST = 1
+HOP = 2
+PLAIN = 6
 AHEAD = 1
 PIECES = 4
 LOADS = 4
@@ -18,10 +20,10 @@
 def swap_kernel(
     sizes,
     d_hbm, c_hbm, run_out, end_out,
-    even, odd, crowd, ghost, edge, below, totals, bases,
+    even, odd, crowd, ghost, edge, below, totals, bases, relay,
     z_send, z_recv, k_send, k_recv, j_send, j_recv,
     in_send, in_recv, in_own, out_send, out_recv, base_send, base_recv,
-    total_send, total_recv,
+    relay_send, relay_recv, total_send, total_recv,
 ):
     n_lat, n_lon, n_lev, nj, ni, nk, cells = sizes
     half, blocks = nk // 2, nj // ROWS
@@ -197,13 +199,123 @@
         theirs = pl.ds(1 + ni * (1 - y_lo), ni)
         return remote(final.at[pl.ds(j + 1, ROWS), theirs], end_out.at[pl.ds(j, ROWS), :, pl.ds(half, half)], out_send.at[block], out_recv.at[block], peer_p)
 
+    def slot(block):
+        return pl.ds(block * ROWS, ROWS)
+
     def total_copy(block):
-        rows = pl.ds(first(block), ROWS)
+        rows = slot(block)
         return remote(totals.at[rows], below.at[rows], total_send.at[block], total_recv.at[block], peer_z)
 
-    def base_copy(block):
-        rows = pl.ds(first(block), ROWS)
-        return remote(bases.at[0, rows], bases.at[1, rows], base_send.at[block], base_recv.at[block], peer_p)
+    far, not_far = pl.ds(0, half // 4), pl.ds(half // 4, half - half // 4)
+    aside, not_aside = pl.ds(0, half // 2), pl.ds(half // 2, half - half // 2)
+    up, down = y_lo == 0, y_lo == 1
+    base_from, base_to = bases.at[0], bases.at[1]
+
+    def base_copy(block, part, source, target, which, arrival, peer):
+        rows = slot(block)
+        return remote(source.at[rows, part], target.at[rows, part], base_send.at[which, block], arrival, peer)
+
+    def relay_copy(block, part, target, which, arrival, peer):
+        rows = slot(block)
+        return remote(relay.at[which, rows, part], target.at[rows, part], relay_send.at[which, block], arrival, peer)
+
+    def give_base_split(block):
+        @pl.when(up)
+        def _():
+            base_copy(block, far, base_from, relay.at[0], 1, relay_recv.at[0, block], peer_j).start()
+            base_copy(block, not_far, base_from, base_to, 0, base_recv.at[0, block], peer_p).start()
+
+        @pl.when(down & (z_hi == 1))
+        def _():
+            base_copy(block, not_aside, base_from, base_to, 0, base_recv.at[0, block], peer_p).start()
+
+        @pl.when(down & (z_hi == 0))
+        def _():
+            base_copy(block, aside, totals, relay.at[1], 1, relay_recv.at[1, block], peer_p).start()
+
+    def relay_first(block):
+        @pl.when(down)
+        def _():
+            copy = relay_copy(block, far, relay.at[0], 0, relay_recv.at[0, block], peer_p)
+            copy.wait_recv()
+            copy.start()
+
+        @pl.when(up & (z_hi == 0))
+        def _():
+            relay_copy(block, aside, relay.at[1], 1, relay_recv.at[1, block], peer_p).wait_recv()
+            relay_copy(block, aside, base_to, 1, base_recv.at[1, block], peer_z).start()
+
+    def relay_second(block):
+        @pl.when(up)
+        def _():
+            relay_copy(block, far, relay.at[0], 0, relay_recv.at[0, block], peer_p).wait_recv()
+            relay_copy(block, far, base_to, 0, base_recv.at[1, block], peer_j).start()
+
+    def wait_base_split(block):
+        @pl.when(down)
+        def _():
+            base_copy(block, not_far, base_from, base_to, 0, base_recv.at[0, block], peer_p).wait_recv()
+            base_copy(block, far, base_from, base_to, 0, base_recv.at[1, block], peer_p).wait_recv()
+
+        @pl.when(up & (z_hi == 1))
+        def _():
+            base_copy(block, not_aside, base_from, base_to, 0, base_recv.at[0, block], peer_p).wait_recv()
+            base_copy(block, aside, base_from, base_to, 0, base_recv.at[1, block], peer_p).wait_recv()
+
+    def sent_base_split(block):
+        relay_copy(block, far, relay.at[0], 0, relay_recv.at[0, block], peer_p).wait_send()
+
+        @pl.when(up)
+        def _():
+            base_copy(block, not_far, base_from, base_to, 0, base_recv.at[0, block], peer_p).wait_send()
+            base_copy(block, far, base_from, base_to, 1, base_recv.at[0, block], peer_p).wait_send()
+
+        @pl.when(up & (z_hi == 0))
+        def _():
+            relay_copy(block, aside, relay.at[1], 1, relay_recv.at[1, block], peer_p).wait_send()
+
+        @pl.when(down & (z_hi == 1))
+        def _():
+            base_copy(block, not_aside, base_from, base_to, 0, base_recv.at[0, block], peer_p).wait_send()
+
+        @pl.when(down & (z_hi == 0))
+        def _():
+            base_copy(block, aside, base_from, base_to, 1, base_recv.at[0, block], peer_p).wait_send()
+
+    every = pl.ds(0, half)
+
+    def give_base_plain(block):
+        @pl.when(up | (z_hi == 1))
+        def _():
+            base_copy(block, every, base_from, base_to, 0, base_recv.at[0, block], peer_p).start()
+
+    def wait_base_plain(block):
+        @pl.when(down | (z_hi == 1))
+        def _():
+            base_copy(block, every, base_from, base_to, 0, base_recv.at[0, block], peer_p).wait_recv()
+
+    def sent_base_plain(block):
+        @pl.when(up | (z_hi == 1))
+        def _():
+            base_copy(block, every, base_from, base_to, 0, base_recv.at[0, block], peer_p).wait_send()
+
+    def either(split, plain, block):
+        @pl.when(block < blocks - PLAIN)
+        def _():
+            split(block)
+
+        @pl.when(block >= blocks - PLAIN)
+        def _():
+            plain(block)
+
+    def give_base(block):
+        either(give_base_split, give_base_plain, block)
+
+    def wait_base(block):
+        either(wait_base_split, wait_base_plain, block)
+
+    def sent_base(block):
+        either(sent_base_split, sent_base_plain, block)
 
     def finish(block):
         out_copy(block).start()
@@ -215,9 +327,13 @@
                 total = final[j + 1, 1]
                 for i in range(1, wide):
                     total = total + final[j + 1, i + 1]
-                totals[j] = total
-                below[j] = jnp.zeros_like(total)
+                totals[block * ROWS + row] = total
+                below[block * ROWS + row] = jnp.zeros_like(total)
             total_copy(block).start()
+
+        @pl.when(up & (z_hi == 0))
+        def _():
+            bases[1, slot(block)] = jnp.zeros((ROWS, half, cells), jnp.float32)
 
     def sums(block):
         @pl.when(z_hi == 1)
@@ -227,23 +343,23 @@
         sent_faces(STEPS - 1, block)
         for row in range(ROWS):
             j = first(block) + row
-            base = below[j]
+            base = below[block * ROWS + row]
             lowest = final[j + 1, 1]
             for i in range(1, ni):
                 lowest = lowest + final[j + 1, i + 1]
-            bases[0, j] = base + jnp.where(y_lo == 0, lowest, 0.0)
-            bases[2, j] = base + jnp.where(y_lo == 1, lowest, 0.0)
-        base_copy(block).start()
+            bases[0, block * ROWS + row] = base + jnp.where(y_lo == 0, lowest, 0.0)
+            bases[2, block * ROWS + row] = base + jnp.where(y_lo == 1, lowest, 0.0)
+        give_base(block)
 
     def returned(block):
         out_copy(block).wait_recv()
-        base_copy(block).wait_recv()
+        wait_base(block)
         for copy in give(block):
             copy.wait_send()
         scale = 1.0 / (ni * n_lon)
         for row in range(ROWS):
             j = first(block) + row
-            run, run_pair = bases[2, j], bases[1, j]
+            run, run_pair = bases[2, block * ROWS + row], bases[1, block * ROWS + row]
             for q in range(ni):
                 value, value_pair = final[j + 1, 1 + ni * y_lo + q], end_out[j, q, half:nk]
                 run, run_pair = run + value, run_pair + value_pair
@@ -253,14 +369,14 @@
                 run_out[j, q, here] = jnp.where(mine, scaled, swing(scaled_pair))
                 run_out[j, q, away] = jnp.where(mine, swing(scaled), scaled_pair)
 
-    def guarded(stage, block):
-        @pl.when((block >= 0) & (block < blocks))
+    def guarded(stage, block, start=0, stop=blocks):
+        @pl.when((block >= start) & (block < stop))
         def _():
             stage(block)
 
     def close(block):
         out_copy(block).wait_send()
-        base_copy(block).wait_send()
+        sent_base(block)
 
         @pl.when(z_hi == 0)
         def _():
@@ -279,7 +395,12 @@
 
     def tick(n, carry):
         prepare(n + AHEAD, 0)
-        guarded(returned, n - LAG * STEPS - 2 * LAST)
+        done = n - LAG * STEPS - LAST
+        split = blocks - PLAIN
+        guarded(relay_second, done - 2 * HOP, stop=split)
+        guarded(relay_first, done - HOP, stop=split)
+        guarded(returned, done - 3 * HOP, stop=split)
+        guarded(returned, done - LAST, start=split)
         guarded(sums, n - LAG * STEPS - LAST)
 
         def last(block):
@@ -292,7 +413,7 @@
         guarded(arrive, n)
         return carry
 
-    lax.fori_loop(0, blocks + LAG * STEPS + 2 * LAST, tick, 0)
+    lax.fori_loop(0, blocks + LAG * STEPS + LAST + max(LAST, 3 * HOP - PLAIN), tick, 0)
     lax.fori_loop(0, blocks, lambda n, _: (close(n), 0)[1], 0)
 
 
@@ -326,11 +447,12 @@
             (nj, half, cells),
             (nj, half, cells),
             (3, nj, half, cells),
+            (2, nj, half, cells),
         ]
         sems = [
             (2, 2, blocks), (2, 2, blocks), (2, 2, blocks), (2, 2, blocks), (2, 2), (2, 2),
-            (2, blocks), (2, blocks), (2, blocks), (blocks,), (blocks,), (blocks,), (blocks,),
-            (blocks,), (blocks,),
+            (2, blocks), (2, blocks), (2, blocks), (blocks,), (blocks,), (2, blocks), (2, blocks),
+            (2, blocks), (2, blocks), (blocks,), (blocks,),
         ]
         sizes = (n_lat, n_lon, n_lev, nj, ni, nk, cells)
         anywhere = pl.BlockSpec(memory_space=pl.ANY)

time: 314 us -> 307 us (0.978)
  Pallas kernels: 313 us -> 304 us
    pallas_call x1, Pallas kernels: 307 us -> 298 us  [body(): pl.pallas_call(kernel, out_shape=(out, out), in_specs=[anywhere, anywhere...]
where the time goes in v4:
time: 307 us; the launch traced here: 304 us
  Pallas kernels  304 us (99%)
    pallas_call x1, Pallas kernels, body(): pl.pallas_call(kernel, out_shape=(out, out), in_specs=[anywhere, anywhere...  298 us

profile of v4, /device:TPU:0, one launch (start us, length us, event | category | flops | bytes accessed | tf_op | source)
XLA Modules:
  0.0 304.4 jit_solution(858708264794641365)
XLA Ops:
  0.6 297.9 %swap_sweep.1 = (f32[32,4,128,128]{3,2,1,0:T(8,128)S(1)}, f32[32,4,128,128]{3,2,1,0:T(8,128)S(1)}) custom-call(f32[32,4,128,128]{3,2,1,0:T(8,128)} %refs_0_.1, f32[32,4,128,128]{3,2,1,0:T(8,128)} %refs_1_.1), custom_call_target="tpu_custom_call" | custom-call | flops 117440512 | bytes 33554432 | tf_op jit(solution)/shard_map/swap_sweep/pallas_call | solution.py:464
  298.5 5.9 %flush.1 = (f32[32,4,128,128]{3,2,1,0:T(8,128)}, f32[32,4,128,128]{3,2,1,0:T(8,128)}) custom-call(f32[32,4,128,128]{3,2,1,0:T(8,128)S(1)} %get-tuple-element.4.run_in, f32[32,4,128,128]{3,2,1,0:T(8,128)S(1)} %get-tuple-element.5.end_in), custom_call_target="tpu_custom_call" | custom-call | flops 2097152 | bytes 33554432 | tf_op jit(solution)/shard_map/flush/pallas_call | solution.py:477
